TPU v7x, 8 devices: a whole 2x2x1 slice. The times are simulated.
8 devices in a mesh: dp: 4 (over z, y, x), pp: 2 (over core).
Axes of the slice: x: 2, y: 2, z: 1, core: 2. Of those that a mesh axis runs over, the one named last changes fastest.
Arguments:
- tokens: int32 [4, 12, 258], P(None, 'dp')
- emb_stack: float32 [2, 50304, 768], P('pp')
- w_up: bfloat16 [2, 1, 768, 3072], P('pp')
- w_down: bfloat16 [2, 1, 3072, 768], P('pp')
- gain_final: bfloat16 [768], replicated
- gain_hid: bfloat16 [768], replicated
- gain_emb: bfloat16 [768], replicated
- gain_mtp: bfloat16 [768], replicated
- w_proj: bfloat16 [1536, 768], replicated
- u_up: bfloat16 [768, 3072], replicated
- u_down: bfloat16 [3072, 768], replicated
- w_out: bfloat16 [768, 50304], replicated
Outputs:
- output 1: float32 [], replicated
- output 2: float32 [2, 50304, 768], P('pp')
- output 3: float32 [2, 1, 768, 3072], P('pp')
- output 4: float32 [2, 1, 3072, 768], P('pp')
All inputs are finite; a program needn't handle non-finite values.
Results may differ from a plain program's by a relative error of at most 0.0194833.
Values are sent between devices in bfloat16 or wider.
A program may use at most 1.75 GiB of HBM per device.

v0:
```python
import functools
import jax
import jax.numpy as jnp
from jax import lax
from jax.sharding import PartitionSpec as P

NORM_EPS = 1e-6
MTP_WEIGHT = 0.3


def rms_plain(values):
    as_wide = values.astype(jnp.float32)
    inv_rms = lax.rsqrt(jnp.mean(as_wide * as_wide, axis=-1, keepdims=True) + NORM_EPS)
    return (as_wide * inv_rms).astype(jnp.bfloat16)


def rms_scale(values, gain_vec):
    as_wide = values.astype(jnp.float32)
    inv_rms = lax.rsqrt(jnp.mean(as_wide * as_wide, axis=-1, keepdims=True) + NORM_EPS)
    return (as_wide * inv_rms * gain_vec.astype(jnp.float32)).astype(jnp.bfloat16)


def mlp_tail(layer_in, normed, w_in, w_back):
    pre_act = jnp.dot(normed, w_in, preferred_element_type=jnp.float32)
    gelu_out = jax.nn.gelu(pre_act).astype(jnp.bfloat16)
    branch = jnp.dot(gelu_out, w_back, preferred_element_type=jnp.float32)
    return (layer_in.astype(jnp.float32) + branch).astype(jnp.bfloat16)


def layer_apply(layer_in, w_in, w_back):
    return mlp_tail(layer_in, rms_plain(layer_in), w_in, w_back)


def token_xent(features, w_out, targets):
    logits = jnp.dot(features, w_out, preferred_element_type=jnp.float32)
    log_norm = jax.nn.logsumexp(logits, axis=-1)
    picked = jnp.take_along_axis(logits, targets[..., None], axis=-1)[..., 0]
    return jnp.sum(log_norm - picked)


def head_loss(hid_rows, nxt_rows, ids_rows, params, loss_scale):
    gain_final, gain_hid, gain_emb, gain_mtp, w_proj, u_up, u_down, w_out = params
    seq_len = hid_rows.shape[-2]
    main_sum = token_xent(rms_scale(hid_rows, gain_final), w_out, ids_rows[..., 1:seq_len + 1])
    joined = jnp.concatenate([rms_scale(hid_rows, gain_hid), rms_scale(nxt_rows, gain_emb)], axis=-1)
    mtp_in = jnp.dot(joined, w_proj, preferred_element_type=jnp.float32).astype(jnp.bfloat16)
    mtp_out = mlp_tail(mtp_in, rms_scale(mtp_in, gain_mtp), u_up, u_down)
    extra_sum = token_xent(rms_scale(mtp_out, gain_final), w_out, ids_rows[..., 2:seq_len + 2])
    return (main_sum + MTP_WEIGHT * extra_sum) * loss_scale


def stage_backward(stage_in, grad_out, up_w, down_w):
    n_layers = up_w.shape[0]
    saved_acts = []
    layer_in = stage_in
    for layer_idx in range(n_layers):
        normed = rms_plain(layer_in)
        pre_act = jnp.dot(normed, up_w[layer_idx], preferred_element_type=jnp.float32)
        gelu_out = jax.nn.gelu(pre_act).astype(jnp.bfloat16)
        saved_acts.append((layer_in, normed, pre_act, gelu_out))
        if layer_idx + 1 < n_layers:
            branch = jnp.dot(gelu_out, down_w[layer_idx], preferred_element_type=jnp.float32)
            layer_in = (layer_in.astype(jnp.float32) + branch).astype(jnp.bfloat16)
    grads_up = []
    grads_down = []
    for layer_idx in reversed(range(n_layers)):
        layer_in, normed, pre_act, gelu_out = saved_acts[layer_idx]
        grads_down.append(jnp.einsum('nf,nh->fh', gelu_out, grad_out, preferred_element_type=jnp.float32))
        grad_gelu = jnp.einsum('nh,fh->nf', grad_out, down_w[layer_idx], preferred_element_type=jnp.float32).astype(jnp.bfloat16)
        gelu_pull = jax.vjp(jax.nn.gelu, pre_act)[1]
        grad_pre = gelu_pull(grad_gelu.astype(jnp.float32))[0].astype(jnp.bfloat16)
        grads_up.append(jnp.einsum('nh,nf->hf', normed, grad_pre, preferred_element_type=jnp.float32))
        grad_normed = jnp.einsum('nf,hf->nh', grad_pre, up_w[layer_idx], preferred_element_type=jnp.float32).astype(jnp.bfloat16)
        norm_pull = jax.vjp(rms_plain, layer_in)[1]
        grad_skip = norm_pull(grad_normed)[0]
        grad_out = (grad_out.astype(jnp.float32) + grad_skip.astype(jnp.float32)).astype(jnp.bfloat16)
    return grad_out, jnp.stack(grads_up[::-1]), jnp.stack(grads_down[::-1])


def solution(mesh):
    n_stages = mesh.shape['pp']
    n_replicas = mesh.shape['dp']
    forward_perm = [(idx, idx + 1) for idx in range(n_stages - 1)]
    backward_perm = [(idx + 1, idx) for idx in range(n_stages - 1)]
    to_last = [(0, n_stages - 1)]
    to_first = [(n_stages - 1, 0)]

    def device_fn(tokens, emb_stack, w_up, w_down, gain_final, gain_hid, gain_emb, gain_mtp, w_proj, u_up, u_down, w_out):
        params = (gain_final, gain_hid, gain_emb, gain_mtp, w_proj, u_up, u_down, w_out)
        n_micro, batch_dev, ids_width = tokens.shape
        seq_len = ids_width - 2
        vocab_size = emb_stack.shape[1]
        hidden = emb_stack.shape[2]
        n_rows = batch_dev * seq_len
        n_ticks = n_micro + n_stages - 1
        inv_total = 1.0 / (n_micro * batch_dev * n_replicas * seq_len)
        stage_idx = lax.axis_index('pp')
        is_first = stage_idx == 0
        is_last = stage_idx == n_stages - 1
        emb_table = emb_stack[0]
        up_w = w_up[0]
        down_w = w_down[0]
        n_layers = up_w.shape[0]
        trunk_ids = tokens[:, :, :seq_len].reshape(n_micro, n_rows)
        next_ids = tokens[:, :, 1:seq_len + 1].reshape(n_micro * n_rows)
        row_ids = tokens.reshape(n_micro * batch_dev, ids_width)

        def fwd_tick(tick_state, tick_idx):
            received, saved_acts = tick_state
            m_here = tick_idx - stage_idx
            is_valid = (m_here >= 0) & (m_here < n_micro)
            m_idx = jnp.clip(m_here, 0, n_micro - 1)
            ids_now = lax.dynamic_index_in_dim(trunk_ids, m_idx, 0, keepdims=False)
            looked_up = jnp.take(emb_table, ids_now, axis=0).astype(jnp.bfloat16)
            stage_in = jnp.where(is_first, looked_up, received)
            old_entry = lax.dynamic_index_in_dim(saved_acts, m_idx, 0, keepdims=False)
            saved_acts = lax.dynamic_update_index_in_dim(saved_acts, jnp.where(is_valid, stage_in, old_entry), m_idx, 0)
            current = stage_in
            for layer_idx in range(n_layers):
                current = layer_apply(current, up_w[layer_idx], down_w[layer_idx])
            received = lax.ppermute(current, 'pp', forward_perm)
            return (received, saved_acts), current

        fwd_init = (jnp.zeros((n_rows, hidden), jnp.bfloat16), jnp.zeros((n_micro, n_rows, hidden), jnp.bfloat16))
        fwd_state, stage_outs = lax.scan(fwd_tick, fwd_init, jnp.arange(n_ticks))
        saved_acts = fwd_state[1]
        final_rows = stage_outs[n_stages - 1:].reshape(n_micro * batch_dev, seq_len, hidden)
        next_rows = jnp.take(emb_table, next_ids, axis=0).astype(jnp.bfloat16).reshape(n_micro * batch_dev, seq_len, hidden)
        next_rows = lax.ppermute(next_rows, 'pp', to_last)

        def head_pass(operands):
            hid_all, nxt_all = operands

            def row_grads(row_item):
                hid_row, nxt_row, ids_row = row_item
                row_fn = functools.partial(head_loss, ids_rows=ids_row, params=params, loss_scale=inv_total)
                row_value, pull_back = jax.vjp(row_fn, hid_row, nxt_row)
                d_hid, d_nxt = pull_back(jnp.ones((), jnp.float32))
                return row_value, d_hid, d_nxt

            row_values, d_hid_all, d_nxt_all = lax.map(row_grads, (hid_all, nxt_all, row_ids))
            return jnp.sum(row_values), d_hid_all, d_nxt_all

        def head_skip(operands):
            hid_all, nxt_all = operands
            return jnp.zeros((), jnp.float32), jnp.zeros_like(hid_all), jnp.zeros_like(nxt_all)

        loss_part, d_final, d_next_rows = lax.cond(is_last, head_pass, head_skip, (final_rows, next_rows))
        d_next = lax.ppermute(d_next_rows, 'pp', to_first)
        d_final_mb = d_final.reshape(n_micro, n_rows, hidden)

        def bwd_tick(tick_state, tick_idx):
            received, acc_up, acc_down = tick_state
            m_here = tick_idx - (n_stages - 1 - stage_idx)
            is_valid = (m_here >= 0) & (m_here < n_micro)
            m_idx = jnp.clip(m_here, 0, n_micro - 1)
            grad_out = jnp.where(is_last, lax.dynamic_index_in_dim(d_final_mb, m_idx, 0, keepdims=False), received)
            stage_in = lax.dynamic_index_in_dim(saved_acts, m_idx, 0, keepdims=False)
            grad_in, grad_up, grad_down = stage_backward(stage_in, grad_out, up_w, down_w)
            acc_up = acc_up + jnp.where(is_valid, grad_up, 0.0)
            acc_down = acc_down + jnp.where(is_valid, grad_down, 0.0)
            received = lax.ppermute(grad_in, 'pp', backward_perm)
            return (received, acc_up, acc_down), grad_in

        bwd_init = (jnp.zeros((n_rows, hidden), jnp.bfloat16), jnp.zeros(up_w.shape, jnp.float32), jnp.zeros(down_w.shape, jnp.float32))
        bwd_state, stage_grads = lax.scan(bwd_tick, bwd_init, jnp.arange(n_ticks))
        first_grads = stage_grads[n_stages - 1:].reshape(n_micro * n_rows, hidden)
        all_rows = jnp.concatenate([first_grads, d_next.reshape(n_micro * n_rows, hidden)]).astype(jnp.float32)
        all_ids = jnp.concatenate([trunk_ids.reshape(n_micro * n_rows), next_ids])
        d_table = jax.ops.segment_sum(all_rows, all_ids, num_segments=vocab_size)
        d_table = lax.psum(jnp.where(is_first, d_table, 0.0), 'dp')
        d_up = lax.psum(bwd_state[1], 'dp')
        d_down = lax.psum(bwd_state[2], 'dp')
        total_loss = lax.psum(loss_part, ('dp', 'pp'))
        return total_loss, d_table[None], d_up[None], d_down[None]

    in_specs = (P(None, 'dp', None), P('pp', None, None), P('pp', None, None, None), P('pp', None, None, None), P(None), P(None), P(None), P(None), P(None, None), P(None, None), P(None, None), P(None, None))
    out_specs = (P(), P('pp', None, None), P('pp', None, None, None), P('pp', None, None, None))
    return jax.shard_map(device_fn, mesh=mesh, in_specs=in_specs, out_specs=out_specs, check_vma=False)
```

profile of v0, /device:TPU:0, one launch (start us, length us, event | category | flops | bytes accessed | tf_op | source)
XLA Modules:
  0.0 7349.9 jit_solution(7664837964651322706)
XLA Ops:
  8.2 55.5 gather_fusion.3
  74.4 73.9 %bitcast_convert_fusion = bf16[50304,768]{1,0:T(8,128)(2,1)} fusion(f32[1,50304,768]{2,1,0:T(8,128)} %param.23), kind=kLoop, calls=%fused_computation.308 | loop fusion | flops 38633472 | bytes 231800832
  153.2 152.0 %while.49 = (s32[]{:T(128)}, bf16[768,768]{1,0:T(8,128)(2,1)}, bf16[4,768,768]{2,1,0:T(8,128)(2,1)}, bf16[5,768,768]{2,1,0:T(8,128)(2,1)}, pred[]{:T(512)}, /*in...) while((s32[]{:T(128)}, bf16[768,768]{1,0:T(8,128)(2,1)}, ...), condition=%wide.region_2.3_spmd, body=%wide.region_0.2_spmd.sunk | while | flops 7276077568 | bytes 35431208 | solution.py:125
  164.3 12.6 bitcast_dynamic-update-slice_fusion.7
  193.0 12.6 bitcast_dynamic-update-slice_fusion.7
  223.7 12.7 bitcast_dynamic-update-slice_fusion.7
  254.7 12.6 bitcast_dynamic-update-slice_fusion.7
  285.5 12.6 bitcast_dynamic-update-slice_fusion.7
  311.6 3439.7 %while.50 = (s32[]{:T(128)}, bf16[768,768]{0,1:T(8,128)(2,1)S(1)}, f32[1,768,3072]{2,1,0:T(8,128)}, f32[1,3072,768]{2,1,0:T(8,128)}, bf16[5,768,768]{1,2,0:T(8,1...) while((s32[]{:T(128)}, bf16[768,768]{0,1:T(8,128)(2,1)S(1)}, ...), condition=%wide.region_27.29_spmd.clone, body=%wide.region_24.28_spmd.clone.sunk | while | flops 18222026752 | bytes 187598736 | solution.py:166
  343.6 11.2 bitcast_add_fusion.5
  363.4 3169.5 %collective-permute-done.1 = bf16[768,768]{0,1:T(8,128)(2,1)S(1)} collective-permute-done((bf16[768,768]{0,1:T(8,128)(2,1)}, bf16[768,768]{0,1:T(8,128)(2,1)S(1)}, u32[]{:S(2)}, u32[]{:S(2)}) %collective-permute-start.1) | collective-permute-done | bytes 1179680 | tf_op jit(solution)/shard_map/while/body/eval_jaxpr/ppermute | solution.py:162
  3564.9 12.6 bitcast_add_fusion.5
  3599.5 10.3 fusion.329
  3619.4 12.6 bitcast_add_fusion.5
  3654.1 10.3 fusion.329
  3674.0 12.6 bitcast_add_fusion.5
  3728.6 12.6 bitcast_add_fusion.5
  3762.8 11.4 maximum_convert_fusion
  3774.3 47.7 broadcast_in_dim.177
  3822.0 792.8 %scatter_fusion = f32[50304,768]{1,0:T(8,128)} fusion(f32[50304,768]{1,0:T(8,128)} %broadcast_in_dim.177, s32[6144]{0:T(1024)S(1)} %copy-done.16, f32[6144,768]{1,0:T(8,128)} %maximum_convert_fusion), kind=kCustom, calls=%fused_computation.4 | custom fusion | flops 4718592 | bytes 56647680 | tf_op jit(solution)/shard_map/scatter-add | solution.py:170
  4614.9 101.3 %select_bitcast_fusion = f32[1,50304,768]{2,1,0:T(8,128)} fusion(f32[50304,768]{1,0:T(8,128)} %scatter_fusion, pred[]{:T(512)} %eq.7), kind=kLoop, calls=%fused_computation.297 | loop fusion | flops 38633472 | bytes 309067776 | tf_op jit(solution)/shard_map/broadcast_in_dim | solution.py:175
  4716.2 25.5 psum.28
  4741.7 2488.0 %all-reduce.4.cloned.1.call-done = f32[1,50304,768]{2,1,0:T(8,128)} async-done(((f32[1,50304,768]{2,1,0:T(8,128)}), f32[1,50304,768]{2,1,0:T(8,128)}) %all-reduce.4.cloned.1.call-update) | async-done | bytes 154533904 | tf_op jit(solution)/shard_map/psum | solution.py:171
  7229.7 100.9 %copy.103 = f32[1,50304,768]{2,1,0:T(8,128)} copy(f32[1,50304,768]{2,1,0:T(8,128)} %all-reduce.4.cloned.1.call-done) | data formatting | bytes 309067776
  (238 shorter events, 320.9 us)
Async XLA Ops:
  7.2 4734.5 %all-reduce.6.cloned.1.call-start = ((), (), s32[]{:S(2)}) async-start(), calls=%async_computation.1 | async-start | bytes 37748736 | tf_op jit(solution)/shard_map/psum | solution.py:172
  69.5 235.6 %collective-permute-start.2 = (bf16[12,256,768]{2,1,0:T(8,128)(2,1)}, bf16[12,256,768]{2,1,0:T(8,128)(2,1)}, u32[]{:S(2)}, u32[]{:S(2)}) collective-permute-start(bf16[12,256,768]{2,1,0:T(8,128)(2,1)} %select_convert_fusion.1), channel_id=1, source_target_pairs={{0,1},{2,3},{4,5},{6,7}} | collective-permute-start | bytes 14155784 | tf_op jit(solution)/shard_map/ppermute | solution.py:129
  177.0 3.7 collective-permute-start
  205.6 5.9 collective-permute-start
  236.4 6.1 collective-permute-start
  267.3 6.0 collective-permute-start
  298.1 6.0 collective-permute-start
  310.2 3452.6 %collective-permute-start.3 = (bf16[12,256,768]{2,1,0:T(8,128)(2,1)}, bf16[12,256,768]{2,1,0:T(8,128)(2,1)}, u32[]{:S(2)}, u32[]{:S(2)}) collective-permute-start(bf16[12,256,768]{2,1,0:T(8,128)(2,1)} %get-tuple-element.451), channel_id=1, source_target_pairs={{1,0},{3,2},{5,4},{7,6}} | collective-permute-start | bytes 14155784 | tf_op jit(solution)/shard_map/ppermute | solution.py:149
  321.1 12.8 copy-start.1
  321.1 12.8 slice-start
  342.3 3190.6 %collective-permute-start.1 = (bf16[768,768]{0,1:T(8,128)(2,1)}, bf16[768,768]{0,1:T(8,128)(2,1)S(1)}, u32[]{:S(2)}, u32[]{:S(2)}) collective-permute-start(bf16[768,768]{0,1:T(8,128)(2,1)} %get-tuple-element.960), channel_id=1, source_target_pairs={{1,0},{3,2},{5,4},{7,6}} | collective-permute-start | bytes 3538952 | tf_op jit(solution)/shard_map/while/body/eval_jaxpr/ppermute | solution.py:162
  3542.4 12.8 copy-start.1
  3563.6 24.0 collective-permute-start.1
  3597.0 12.8 copy-start.1
  3597.1 12.8 slice-start
  3618.1 24.0 collective-permute-start.1
  3651.6 12.8 copy-start.1
  3651.6 12.8 slice-start
  3672.7 24.0 collective-permute-start.1
  3706.2 12.8 copy-start.1
  3706.2 12.8 slice-start
  3727.3 24.0 collective-permute-start.1
  3762.8 3466.9 %all-reduce.4.cloned.1.call-start = ((), (), s32[]{:S(2)}) async-start(), calls=%async_computation | async-start | bytes 309067776 | tf_op jit(solution)/shard_map/psum | solution.py:171
  3774.3 47.7 copy-start.16
  (22 other events, 164.1 us)
Sparse Core Ops, SparseCore 0:
  3762.9 349.5 all-reduce.5
  4716.3 2513.3 all-reduce.3
where the time goes:
time: 7400 us; the launch traced here: 7350 us
  waiting for transfers between devices  5670 us (77%)
  other arithmetic  1020 us (14%)
  local copies, waits for them, and re-layouts  299 us (4%)
  matrix products  286 us (4%)
    ppermute x5, waiting for transfers between devices, bwd_tick(): received = lax.ppermute(grad_in, 'pp', backward_perm)  3170 us
    psum x1, waiting for transfers between devices, device_fn(): d_table = lax.psum(jnp.where(is_first, d_table, 0.0), 'dp')  2490 us
    scatter-add x1, other arithmetic, device_fn(): d_table = jax.ops.segment_sum(all_rows, all_ids, num_segments=vocab_size)  793 us
  transfers between devices with their start and end apart: 14, of which 7 were waited for; matrix products, arithmetic and copies ran while one was open for 19% of the time, Pallas kernels for 0%

commit v1 on v0

v1 whole, which is shorter than its diff:
```python
import functools
import jax
import jax.numpy as jnp
from jax import lax
from jax.experimental import pallas as pl
from jax.experimental.pallas import tpu as pltpu
from jax.sharding import PartitionSpec as P

NORM_EPS = 1e-6
MTP_WEIGHT = 0.3
LOG2E = 1.4426950408889634
LN2 = 0.6931471805599453
VB = 1024
RC = 256
TAIL = 128
TB = 384
KW = 16
F32 = jnp.float32
BF16 = jnp.bfloat16


def rms_plain(values):
    as_wide = values.astype(F32)
    inv_rms = lax.rsqrt(jnp.mean(as_wide * as_wide, axis=-1, keepdims=True) + NORM_EPS)
    return (as_wide * inv_rms).astype(BF16)


def rms_scale(values, gain_vec):
    as_wide = values.astype(F32)
    inv_rms = lax.rsqrt(jnp.mean(as_wide * as_wide, axis=-1, keepdims=True) + NORM_EPS)
    return (as_wide * inv_rms * gain_vec.astype(F32)).astype(BF16)


def dot(a, b):
    return jnp.dot(a, b, preferred_element_type=F32)


def dot_nt(a, b):
    return lax.dot_general(a, b, (((1,), (1,)), ((), ())), preferred_element_type=F32)


def dot_tn(a, b):
    return lax.dot_general(a, b, (((0,), (0,)), ((), ())), preferred_element_type=F32)


def add_bf16(a, b):
    return (a.astype(F32) + b.astype(F32)).astype(BF16)


def mlp_forward(layer_in, normed, w_in, w_back):
    pre_act = dot(normed, w_in)
    gelu_out = jax.nn.gelu(pre_act).astype(BF16)
    out = (layer_in.astype(F32) + dot(gelu_out, w_back)).astype(BF16)
    return out, pre_act, gelu_out


def mlp_backward(grad_out, pre_act, w_in, w_back):
    grad_gelu = dot_nt(grad_out, w_back).astype(BF16)
    grad_pre = jax.vjp(jax.nn.gelu, pre_act)[1](grad_gelu.astype(F32))[0].astype(BF16)
    return grad_pre, dot_nt(grad_pre, w_in).astype(BF16)


def rank_of(ids):
    n = ids.shape[-1]
    key = ids * n + lax.iota(jnp.int32, n)
    return jnp.sum((key[..., None, :] < key[..., :, None]).astype(jnp.int32), axis=-1)


def sort_by_rank(ids, rank):
    n = ids.shape[-1]
    hit = rank[..., None, :] == lax.iota(jnp.int32, n)[:, None]
    return jnp.sum(jnp.where(hit, ids[..., None, :], 0), axis=-1)


def sort_rows(rows, rank):
    n = rank.shape[-1]
    hit = rank[None, :] == lax.iota(jnp.int32, n)[:, None]
    return dot(hit.astype(BF16), rows).astype(BF16)


def prep_kernel(info, ids, off, emb_ref, w_ref, wt_ref, tgt_ref, rows_ref, out_ref, buf, acc, sems, *, group, n_pad, n_blocks):
    step = pl.program_id(0)
    is_first = info[0] == 0

    @pl.when(is_first)
    def _():
        slot = lax.rem(step, 2)

        def start(j, _):
            row = ids[step * group + j]
            pltpu.make_async_copy(emb_ref.at[0, pl.ds(row, 1), :], buf.at[slot, pl.ds(j, 1), :], sems.at[slot]).start()
            return 0

        lax.fori_loop(0, group, start, 0, unroll=8)

        def finish(which, base):
            pltpu.make_async_copy(buf.at[which], buf.at[which], sems.at[which]).wait()
            rows_ref[pl.ds(pl.multiple_of(base, 16), group), :] = buf[which].astype(BF16)

        @pl.when(step > 0)
        def _():
            finish(1 - slot, (step - 1) * group)

        @pl.when(step == n_blocks - 1)
        def _():
            finish(slot, step * group)

    @pl.when(jnp.logical_not(is_first))
    def _():
        @pl.when(step == 0)
        def _():
            acc[...] = jnp.zeros_like(acc)

        lane = lax.broadcasted_iota(jnp.int32, (128, 128), 1)

        def extract(block, base, w_block):
            width = w_block.shape[1]
            begins, counts = [], []
            for side in range(2):
                begin = off[side, block]
                end = off[side, block + 1]
                begin16 = (begin // 16) * 16
                begins.append(begin16)
                counts.append(jnp.where(end > begin, (end - begin16 + 127) // 128, 0))

            def body(it, _):
                starts = [pl.multiple_of(jnp.minimum(b + it * 128, n_pad), 16) for b in begins]
                hot = []
                for side in range(2):
                    rel = tgt_ref[side, pl.ds(starts[side], 128), :] - base
                    hot.append(jnp.concatenate([jnp.where(rel - 128 * j == lane, 1.0, 0.0).astype(BF16) for j in range(width // 128)], axis=1))
                picked = dot_nt(jnp.concatenate(hot, axis=0), w_block[...])
                for side in range(2):
                    acc[side, pl.ds(starts[side], 128), :] += picked[side * 128:(side + 1) * 128]
                return 0

            lax.fori_loop(0, jnp.maximum(counts[0], counts[1]), body, 0)

        extract(step, step * VB, w_ref)

        @pl.when(step == n_blocks - 1)
        def _():
            extract(n_blocks, n_blocks * VB, wt_ref)
            out_ref[...] = acc[:, :n_pad, :].astype(BF16)


def prep(core, ids, off, emb_stack, w_out, w_tail, tgt_wide):
    hidden, vocab = w_out.shape
    n_blocks = vocab // VB
    n_pad = ids.shape[0] // 2
    group = ids.shape[0] // n_blocks
    whole = pl.Buffered(1)

    return pl.pallas_call(
        functools.partial(prep_kernel, group=group, n_pad=n_pad, n_blocks=n_blocks),
        grid_spec=pltpu.PrefetchScalarGridSpec(
            num_scalar_prefetch=3,
            grid=(n_blocks,),
            in_specs=[
                pl.BlockSpec(memory_space=pl.ANY),
                pl.BlockSpec((hidden, VB), lambda v, *_: (0, v)),
                pl.BlockSpec((hidden, TAIL), lambda v, *_: (0, 0), pipeline_mode=whole),
                pl.BlockSpec(tgt_wide.shape, lambda v, *_: (0, 0, 0), pipeline_mode=whole),
            ],
            out_specs=[
                pl.BlockSpec((2 * n_pad, hidden), lambda v, *_: (0, 0)),
                pl.BlockSpec((2, n_pad, hidden), lambda v, *_: (0, 0, 0)),
            ],
            scratch_shapes=[
                pltpu.VMEM((2, group, hidden), F32),
                pltpu.VMEM((2, n_pad + 128, hidden), F32),
                pltpu.SemaphoreType.DMA((2,)),
            ],
        ),
        out_shape=[
            jax.ShapeDtypeStruct((2 * n_pad, hidden), BF16),
            jax.ShapeDtypeStruct((2, n_pad, hidden), BF16),
        ],
        compiler_params=pltpu.CompilerParams(vmem_limit_bytes=48 * 2**20, dimension_semantics=("arbitrary",)),
        cost_estimate=pl.CostEstimate(flops=10**10, bytes_accessed=10**8, transcendentals=0),
        name="prep",
    )(core, ids, off, emb_stack, w_out, w_tail, tgt_wide)


def heads_kernel(x_ref, wt_ref, w_ref, w_any, acc_ref, l_ref, m_ref, s0, s1, p0, p1, sem, *, n_blocks):
    step = pl.program_id(0)
    n_chunks = x_ref.shape[0] // RC

    def rows_of(r):
        return pl.ds(pl.multiple_of(r * RC, RC), RC)

    def logits(r, s_ref):
        s_ref[...] = dot(x_ref[rows_of(r), :], w_ref[...])

    def weights(r, s_ref, p_ref):
        top = m_ref[rows_of(r), :]
        total = l_ref[rows_of(r), :]
        for j in range(VB // 128):
            cols = slice(j * 128, (j + 1) * 128)
            e = jnp.exp2(s_ref[:, cols] * LOG2E - top)
            total = total + e
            p_ref[:, cols] = e.astype(BF16)
        l_ref[rows_of(r), :] = total

    def gather(r, p_ref):
        acc_ref[rows_of(r), :] += dot_nt(p_ref[...], w_ref[...])

    def start_rows(r, _):
        s = dot(x_ref[rows_of(r), :], wt_ref[...]) * LOG2E
        top = jnp.max(s, axis=1, keepdims=True)
        e = jnp.exp2(s - top)
        m_ref[rows_of(r), :] = jnp.broadcast_to(top, (RC, 128))
        l_ref[rows_of(r), :] = e
        acc_ref[rows_of(r), :] = dot_nt(e.astype(BF16), wt_ref[...])
        return 0

    @pl.when(step == 0)
    def _():
        lax.fori_loop(0, n_chunks, start_rows, 0)

    logits(0, s0)

    def pair(i, _):
        r = 2 * i
        logits(r + 1, s1)
        weights(r, s0, p0)
        gather(r, p0)
        logits(lax.rem(r + 2, n_chunks), s0)
        weights(r + 1, s1, p1)
        gather(r + 1, p1)
        return 0

    lax.fori_loop(0, n_chunks // 2, pair, 0)

    @pl.when(step == n_blocks - 1)
    def _():
        top_sum = jnp.max(jnp.where(l_ref[...] < 1e30, 0.0, 1.0))

        @pl.when(top_sum > 0.0)
        def _():
            lax.fori_loop(0, n_chunks, start_rows, 0)

            def block(v, _):
                copy = pltpu.make_async_copy(w_any.at[:, pl.ds(pl.multiple_of(v * VB, VB), VB)], w_ref, sem)
                copy.start()
                copy.wait()

                def redo(r, _):
                    rows = rows_of(r)
                    s = dot(x_ref[rows, :], w_ref[...]) * LOG2E
                    old = m_ref[rows, :]
                    new = jnp.maximum(old, jnp.max(s, axis=1, keepdims=True))
                    shrink = jnp.exp2(old - new)
                    e = jnp.exp2(s - new[:, :1])
                    total = l_ref[rows, :] * shrink
                    for j in range(VB // 128):
                        total = total + e[:, j * 128:(j + 1) * 128]
                    l_ref[rows, :] = total
                    m_ref[rows, :] = new
                    acc_ref[rows, :] = acc_ref[rows, :] * shrink[:, :1] + dot_nt(e.astype(BF16), w_ref[...])
                    return 0

                lax.fori_loop(0, n_chunks, redo, 0)
                return 0

            lax.fori_loop(0, n_blocks, block, 0)


def heads(x, w_out, w_tail):

    rows, hidden = x.shape
    n_blocks = w_out.shape[1] // VB
    whole = pl.Buffered(1)
    fixed = lambda v: (0, 0)
    flops = 4 * rows * hidden * w_out.shape[1]
    return pl.pallas_call(
        functools.partial(heads_kernel, n_blocks=n_blocks),
        grid=(n_blocks,),
        in_specs=[
            pl.BlockSpec((rows, hidden), fixed, pipeline_mode=whole),
            pl.BlockSpec((hidden, TAIL), fixed, pipeline_mode=whole),
            pl.BlockSpec((hidden, VB), lambda v: (0, v)),
            pl.BlockSpec(memory_space=pl.ANY),
        ],
        out_specs=[
            pl.BlockSpec((rows, hidden), fixed),
            pl.BlockSpec((rows, 128), fixed),
            pl.BlockSpec((rows, 128), fixed),
        ],
        out_shape=[
            jax.ShapeDtypeStruct((rows, hidden), F32),
            jax.ShapeDtypeStruct((rows, 128), F32),
            jax.ShapeDtypeStruct((rows, 128), F32),
        ],
        scratch_shapes=[
            pltpu.VMEM((RC, VB), F32),
            pltpu.VMEM((RC, VB), F32),
            pltpu.VMEM((RC, VB), BF16),
            pltpu.VMEM((RC, VB), BF16),
            pltpu.SemaphoreType.DMA,
        ],
        compiler_params=pltpu.CompilerParams(vmem_limit_bytes=60 * 2**20, dimension_semantics=("arbitrary",)),
        cost_estimate=pl.CostEstimate(flops=flops, bytes_accessed=10**8, transcendentals=rows * w_out.shape[1]),
        name="heads",
    )(x, w_tail, w_out, w_out)


def table_kernel(blk, first, n_groups, sched_a, sched_b, src_a, src_b, ids_a, ids_b, out_ref, kbuf, ibuf, sems):
    step = pl.program_id(0)
    count = n_groups[0]
    slot = lax.rem(step, 2)

    def copies(which, group):
        made = []
        for side, (sched, src, ids) in enumerate(((sched_a, src_a, ids_a), (sched_b, src_b, ids_b))):
            for k in range(KW):
                index = sched[group * KW + k]
                to = pl.ds((side * KW + k) * 16, 16)
                from_src = pl.ds(pl.multiple_of(jnp.minimum(index * 16, src.shape[0] - 16), 16), 16)
                from_ids = pl.ds(pl.multiple_of(index * 16, 16), 16)
                made.append(pltpu.make_async_copy(src.at[from_src, :], kbuf.at[which, to, :], sems.at[which]))
                made.append(pltpu.make_async_copy(ids.at[from_ids, :], ibuf.at[which, to, :], sems.at[which]))
        return made

    @pl.when((step == 0) & (count > 0))
    def _():
        for copy in copies(0, 0):
            copy.start()

    @pl.when(step + 1 < count)
    def _():
        for copy in copies(1 - slot, step + 1):
            copy.start()

    @pl.when(first[step] == 1)
    def _():
        out_ref[...] = jnp.zeros_like(out_ref)

    @pl.when(step < count)
    def _():
        pltpu.make_async_copy(kbuf.at[slot], kbuf.at[slot], sems.at[slot]).wait()
        pltpu.make_async_copy(ibuf.at[slot], ibuf.at[slot], sems.at[slot]).wait()
        rel = ibuf[slot] - blk[step] * TB
        lane = lax.broadcasted_iota(jnp.int32, rel.shape, 1)
        hot = jnp.concatenate([jnp.where(rel - 128 * j == lane, 1.0, 0.0).astype(BF16) for j in range(TB // 128)], axis=1)
        out_ref[0] += dot_tn(hot, kbuf[slot])


def table(blk, first, n_groups, sched_a, sched_b, src_a, src_b, ids_a, ids_b, vocab):
    hidden = src_a.shape[1]
    n_steps = blk.shape[0]
    anywhere = pl.BlockSpec(memory_space=pl.ANY)
    return pl.pallas_call(
        table_kernel,
        grid_spec=pltpu.PrefetchScalarGridSpec(
            num_scalar_prefetch=5,
            grid=(n_steps,),
            in_specs=[anywhere] * 4,
            out_specs=pl.BlockSpec((1, TB, hidden), lambda s, blk, *_: (0, blk[s], 0)),
            scratch_shapes=[
                pltpu.VMEM((2, 2 * KW * 16, hidden), BF16),
                pltpu.VMEM((2, 2 * KW * 16, 128), jnp.int32),
                pltpu.SemaphoreType.DMA((2,)),
            ],
        ),
        out_shape=jax.ShapeDtypeStruct((1, vocab, hidden), F32),
        compiler_params=pltpu.CompilerParams(vmem_limit_bytes=48 * 2**20, dimension_semantics=("arbitrary",)),
        cost_estimate=pl.CostEstimate(flops=6 * 10**10, bytes_accessed=2 * 10**8, transcendentals=0),
        name="table",
    )(blk, first, n_groups, sched_a, sched_b, src_a, src_b, ids_a, ids_b)


def plan_table(ids_a, ids_b, vocab, active):
    n_blocks = vocab // TB
    n_lists, n = ids_a.shape
    edges = lax.iota(jnp.int32, n_blocks + 1) * TB
    per_list = n // 16
    counts, starts = [], []
    for ids in (ids_a, ids_b):
        off = jnp.sum((ids[:, None, :] < edges[None, :, None]).astype(jnp.int32), axis=-1)
        begin, end = off[:, :-1], off[:, 1:]
        count = jnp.where(end > begin, (end + 15) // 16 - begin // 16, 0) * active
        counts.append(count.T)
        starts.append((begin // 16 + lax.iota(jnp.int32, n_lists)[:, None] * per_list).T)
    need = jnp.maximum(jnp.sum(counts[0], 1), jnp.sum(counts[1], 1))
    groups = jnp.maximum((need + KW - 1) // KW, 1)
    upto = jnp.sum(jnp.where(lax.iota(jnp.int32, n_blocks)[None, :] <= lax.iota(jnp.int32, n_blocks)[:, None], groups[None, :], 0), 1)
    base = upto - groups
    total = upto[-1]
    max_groups = plan_steps(n_lists, n, vocab)
    g_idx = lax.iota(jnp.int32, max_groups)
    blk = jnp.minimum(jnp.sum((upto[None, :] <= g_idx[:, None]).astype(jnp.int32), 1), n_blocks - 1)
    first = jnp.sum((base[None, :] == g_idx[:, None]).astype(jnp.int32), 1)
    scheds = []
    slots = lax.iota(jnp.int32, max_groups * KW)
    dummy = n_lists * per_list
    lower = (lax.iota(jnp.int32, n_lists)[:, None] < lax.iota(jnp.int32, n_lists)[None, :]).astype(jnp.int32)
    for count, start in zip(counts, starts):
        before = jnp.sum(count[:, :, None] * lower[None], axis=1)
        q = ((base * KW)[:, None] + before).reshape(-1)
        c = count.reshape(-1)
        w = start.reshape(-1)
        rel = slots[:, None] - q[None, :]
        inside = (rel >= 0) & (rel < c[None, :])
        scheds.append(jnp.sum(jnp.where(inside, w[None, :] + rel - dummy, 0), 1) + dummy)
    return blk, first, jnp.reshape(total * active, (1,)), scheds[0], scheds[1]


def plan_steps(n_lists, n, vocab):
    n_blocks = vocab // TB
    return 2 * ((n_lists * (n // 16 + n_blocks)) // KW) + n_blocks


def solution(mesh):
    n_stages = mesh.shape['pp']
    n_replicas = mesh.shape['dp']

    def device_fn(tokens, emb_stack, w_up, w_down, gain_final, gain_hid, gain_emb, gain_mtp, w_proj, u_up, u_down, w_out):
        n_micro, batch_dev, ids_width = tokens.shape
        seq_len = ids_width - 2
        vocab, hidden = emb_stack.shape[1:]
        ffn = w_up.shape[-1]
        n_seq = n_micro * batch_dev
        half = n_seq // 2
        n_pos = half * seq_len
        inv_total = 1.0 / (n_seq * n_replicas * seq_len)
        core = lax.axis_index('pp')
        is_first = core == 0
        n_blocks = vocab // VB
        w_tail = w_out[:, n_blocks * VB:]

        seqs = tokens.reshape(2, half, ids_width)
        span = seq_len + 1
        n_slots = half * span
        per_step = -(-n_slots // (n_blocks * 16)) * 16
        n_pad = per_step * n_blocks
        fill = ((0, 0), (0, n_pad - n_slots))
        emb_ids = jnp.pad(seqs[:, :, :span].reshape(2, n_slots), fill)
        targets = jnp.pad(seqs[:, :, 1:].reshape(2, n_slots), fill, constant_values=vocab)
        t_rank = rank_of(targets)
        t_sorted = sort_by_rank(targets, t_rank)
        edges = jnp.minimum(lax.iota(jnp.int32, n_blocks + 2) * VB, vocab)
        off = jnp.sum((t_sorted[:, None, :] < edges[None, :, None]).astype(jnp.int32), axis=-1)
        tgt_wide = jnp.broadcast_to(jnp.pad(t_sorted, ((0, 0), (0, 128)), constant_values=vocab)[:, :, None], (2, n_pad + 128, 128))

        emb_rows, wt_rows = prep(jnp.reshape(core, (1,)), emb_ids.reshape(-1), off, emb_stack, w_out, w_tail, tgt_wide)
        emb_rows = emb_rows.reshape(2, n_pad, hidden)
        swap = [(0, 1), (1, 0)]
        got = lax.ppermute(jnp.where(is_first, emb_rows[1], wt_rows[0]), 'pp', swap)
        own_emb = jnp.where(is_first, emb_rows[0], got)
        own_wt = jnp.where(is_first, got, wt_rows[1])
        own_rank = jnp.where(is_first, t_rank[0], t_rank[1])
        own_seqs = jnp.where(is_first, seqs[0], seqs[1])

        own_emb = own_emb[:n_slots].reshape(half, span, hidden)
        x0 = own_emb[:, :seq_len].reshape(n_pos, hidden)
        e1 = own_emb[:, 1:].reshape(n_pos, hidden)
        hit = own_rank[:n_slots, None] == lax.iota(jnp.int32, n_pad)[None, :]
        wt_slots = dot(hit.astype(BF16), own_wt).astype(BF16).reshape(half, span, hidden)
        wt_main = wt_slots[:, :seq_len].reshape(n_pos, hidden)
        wt_mtp = wt_slots[:, 1:].reshape(n_pos, hidden)

        up_both = lax.all_gather(w_up[0, 0], 'pp')
        down_both = lax.all_gather(w_down[0, 0], 'pp')
        stage_in = x0
        saved = []
        for stage in range(n_stages):
            normed = rms_plain(stage_in)
            out, pre_act, gelu_out = mlp_forward(stage_in, normed, up_both[stage], down_both[stage])
            saved.append((stage_in, normed, pre_act, gelu_out))
            stage_in = out
        hid = stage_in

        def joined_of(h, e):
            return jnp.concatenate([rms_scale(h, gain_hid), rms_scale(e, gain_emb)], axis=-1)

        feat_main, pull_main = jax.vjp(lambda h: rms_scale(h, gain_final), hid)
        joined, pull_joined = jax.vjp(joined_of, hid, e1)
        mtp_in = dot(joined, w_proj).astype(BF16)
        mtp_normed, pull_mtp = jax.vjp(lambda z: rms_scale(z, gain_mtp), mtp_in)
        mtp_out, mtp_pre, _ = mlp_forward(mtp_in, mtp_normed, u_up, u_down)
        feat_mtp, pull_out = jax.vjp(lambda z: rms_scale(z, gain_final), mtp_out)

        feats = jnp.concatenate([feat_main, feat_mtp])
        acc, sums, tops = heads(feats, w_out, w_tail)
        total = jnp.sum(sums, axis=1, keepdims=True)
        scale = jnp.concatenate([jnp.full((n_pos, 1), inv_total, F32), jnp.full((n_pos, 1), MTP_WEIGHT * inv_total, F32)])
        wt = jnp.concatenate([wt_main, wt_mtp])
        picked = jnp.sum(feats.astype(F32) * wt.astype(F32), axis=1, keepdims=True)
        log_norm = (tops[:, :1] + jnp.log2(total)) * LN2
        loss_part = jnp.sum((log_norm - picked) * scale)
        d_feats = ((acc / total - wt.astype(F32)) * scale).astype(BF16)

        d_mtp_out = pull_out(d_feats[n_pos:])[0]
        _, d_mtp_normed = mlp_backward(d_mtp_out, mtp_pre, u_up, u_down)
        d_mtp_in = add_bf16(d_mtp_out, pull_mtp(d_mtp_normed)[0])
        d_joined = dot_nt(d_mtp_in, w_proj).astype(BF16)
        d_hid, d_e1 = pull_joined(d_joined)
        grad = d_hid + pull_main(d_feats[:n_pos])[0]

        d_ups, d_downs = [], []
        for stage in reversed(range(n_stages)):
            stage_in, normed, pre_act, gelu_out = saved[stage]
            d_downs.append(dot_tn(gelu_out, grad))
            grad_pre, d_normed = mlp_backward(grad, pre_act, up_both[stage], down_both[stage])
            d_ups.append(dot_tn(normed, grad_pre))
            grad = add_bf16(grad, jax.vjp(rms_plain, stage_in)[1](d_normed)[0])

        grad_ids = jnp.stack([own_seqs[:, :seq_len].reshape(n_pos), own_seqs[:, 1:seq_len + 1].reshape(n_pos)])
        g_rank = rank_of(grad_ids)
        g_sorted = sort_by_rank(grad_ids, g_rank)
        mine = jnp.concatenate([sort_rows(grad, g_rank[0]), sort_rows(d_e1, g_rank[1])])
        all_ids = lax.all_gather(lax.all_gather(g_sorted, 'dp'), 'pp').reshape(2, n_replicas * 2, n_pos)
        gathered = lax.all_gather(mine, 'dp', tiled=True)
        other = lax.ppermute(gathered, 'pp', [(1, 0)])
        plan = plan_table(all_ids[0], all_ids[1], vocab, jnp.where(is_first, 1, 0))
        pad_ids = [jnp.pad(a.reshape(-1), (0, 16), constant_values=-1) for a in (all_ids[0], all_ids[1])]
        wide = [jnp.broadcast_to(a[:, None], (a.shape[0], 128)) for a in pad_ids]
        d_table = table(*plan, gathered, other, wide[0], wide[1], vocab)

        d_up = jnp.stack(d_ups[::-1])
        d_down = jnp.stack(d_downs[::-1])
        d_up, d_down, _ = lax.optimization_barrier((d_up, d_down, other[:8]))
        d_up = lax.psum_scatter(d_up, 'pp', scatter_dimension=0, tiled=True)
        d_down = lax.psum_scatter(d_down, 'pp', scatter_dimension=0, tiled=True)
        d_up = lax.psum(d_up, 'dp')
        d_down = lax.psum(d_down, 'dp')
        total_loss = lax.psum(loss_part, ('dp', 'pp'))
        return total_loss, d_table, d_up[None], d_down[None]

    in_specs = (P(None, 'dp', None), P('pp', None, None), P('pp', None, None, None), P('pp', None, None, None), P(None), P(None), P(None), P(None), P(None, None), P(None, None), P(None, None), P(None, None))
    out_specs = (P(), P('pp', None, None), P('pp', None, None, None), P('pp', None, None, None))
    return jax.shard_map(device_fn, mesh=mesh, in_specs=in_specs, out_specs=out_specs, check_vma=False)
```

time: 7400 us -> 1600 us (0.22)
  waiting for transfers between devices: 5670 us -> 248 us
  other arithmetic: 1020 us -> 103 us
  Pallas kernels: 0 us -> 847 us
  local copies, waits for them, and re-layouts: 299 us -> 57.7 us
    ppermute x12 -> x2, waiting for transfers between devices: 3180 us -> 0.01 us  [the longest x1 0.01 us: device_fn(): got = lax.ppermute(jnp.where(is_first, emb_rows[1], wt_rows[0]), 'pp', swap)]
    psum x2 -> x1, waiting for transfers between devices: 2490 us -> 83.8 us  [device_fn(): d_up = lax.psum(d_up, 'dp')]
    pallas_call x0 -> x3, Pallas kernels: none -> 847 us  [the longest x1 625 us: heads(): pl.pallas_call(functools.partial(heads_kernel, n_blocks=n_blocks), grid=(...]
    scatter-add x1 -> x0, other arithmetic: 793 us -> none  [device_fn(): d_table = jax.ops.segment_sum(all_rows, all_ids, num_segments=vocab_size)]
    all_gather x0 -> x3, waiting for transfers between devices: none -> 101 us  [the longest x1 101 us: device_fn(): gathered = lax.all_gather(mine, 'dp', tiled=True)]
    broadcast_in_dim x1 -> x0, other arithmetic: 101 us -> none  [device_fn(): return (total_loss, d_table[None], d_up[None], d_down[None])]
    unnamed x7 -> x152, local copies, waits for them, and re-layouts: 113 us -> 21.4 us
    gather x6 -> x0, local copies, waits for them, and re-layouts: 84 us -> none  [the longest x1 55.5 us: device_fn(): jnp.take(emb_table, next_ids, axis=0).astype(jnp.bfloat16)]
  transfers between devices with their start and end apart: 14 -> 8, of which waited for: 7 -> 4; matrix products, arithmetic and copies ran while one was open for 19% -> 12% of each run, Pallas kernels for 0% -> 14%
where the time goes in v1:
time: 1600 us; the launch traced here: 1580 us
  Pallas kernels  847 us (53%)
  matrix products  268 us (17%)
  waiting for transfers between devices  248 us (16%)
  other arithmetic  103 us (6%)
  local copies, waits for them, and re-layouts  57.7 us (4%)
  blocking collectives  34.3 us (2%)
  between operations  16.6 us (1%)
    pallas_call x1, Pallas kernels, heads(): pl.pallas_call(functools.partial(heads_kernel, n_blocks=n_blocks), grid=(...  625 us
    pallas_call x1, Pallas kernels, table(): pl.pallas_call(table_kernel, grid_spec=pltpu.PrefetchScalarGridSpec(num_s...  168 us
    dot_general x10, matrix products, dot(): return jnp.dot(a, b, preferred_element_type=F32)  110 us
    dot_general x6, matrix products, dot_nt(): lax.dot_general(a, b, (((1,), (1,)), ((), ())), preferred_element_type=F32)  106 us
    all_gather x1, waiting for transfers between devices, device_fn(): gathered = lax.all_gather(mine, 'dp', tiled=True)  101 us
    psum x1, waiting for transfers between devices, device_fn(): d_up = lax.psum(d_up, 'dp')  83.8 us
    pallas_call x1, Pallas kernels, prep(): pl.pallas_call(functools.partial(prep_kernel, group=group, n_pad=n_pad, n...  53.7 us
    dot_general x4, matrix products, dot_tn(): lax.dot_general(a, b, (((0,), (0,)), ((), ())), preferred_element_type=F32)  52.3 us
  transfers between devices with their start and end apart: 8, of which 4 were waited for; matrix products, arithmetic and copies ran while one was open for 12% of the time, Pallas kernels for 14%

profile of v1, /device:TPU:0, one launch (start us, length us, event | category | flops | bytes accessed | tf_op | source)
XLA Modules:
  0.0 1584.1 jit_solution(8494746487277151660)
XLA Ops:
  16.9 53.7 %prep.1 = (bf16[3136,768]{1,0:T(8,128)(2,1)}, bf16[2,1568,768]{2,1,0:T(8,128)(2,1)}) custom-call(s32[1]{0:T(128)} %bitcast.info, s32[3136]{0:T(1024)S(1)} %reshape.384.ids, s32[2,51]{1,0:T(2,128)S(1)} %copy.68.off, f32[1,50304,768]{2,1,0:T(8,128)} %emb_ref.1, bf16[768,50304]{1,0:T(8,128)(2,1)} %w_any.1, bf16[768,128]{1,0:T(8,128)(2,1)S(1)} %slice.123.wt_ref, ...), custom_call_target="tpu_custom_call" | custom-call | flops 10000000000 | bytes 100000000 | tf_op jit(solution)/shard_map/prep/pallas_call | solution.py:154
  123.2 13.8 fusion.89
  137.1 16.6 %fusion.62 = (f32[1536]{0:T(1024)S(1)}, bf16[1536,768]{1,0:T(8,128)(2,1)S(1)}) fusion(bf16[2,1,3072,768]{3,2,1,0:T(8,128)(2,1)} %all-gather.13.cloned.1.call-done, f32[1536,3072]{1,0:T(8,128)} %fusion.89, bf16[6,256,768]{2,1,0:T(8,128)(2,1)} %slice.167), kind=kOutput, calls=%fused_computation.133 | convolution fusion | flops 7297300992 | bytes 28317696 | tf_op jit(solution)/shard_map/dot_general | solution.py:35
  153.7 14.0 fusion.92
  167.7 16.4 %fusion.71 = (f32[1536]{0:T(1024)S(1)}, bf16[1536,768]{1,0:T(8,128)(2,1)S(1)}) fusion(bf16[2,1,3072,768]{3,2,1,0:T(8,128)(2,1)} %all-gather.13.cloned.1.call-done, f32[1536,3072]{1,0:T(8,128)} %fusion.92, bf16[1536,768]{1,0:T(8,128)(2,1)S(1)} %get-tuple-element.72), kind=kOutput, calls=%fused_computation.142 | convolution fusion | flops 7297300992 | bytes 28317696 | tf_op jit(solution)/shard_map/dot_general | solution.py:35
  193.1 11.0 fusion.107
  204.1 15.8 fusion.58
  225.9 624.9 %heads.1 = (f32[3072,768]{1,0:T(8,128)}, f32[3072,128]{1,0:T(8,128)}, f32[3072,128]{1,0:T(8,128)}) custom-call(bf16[3072,768]{1,0:T(8,128)(2,1)} %pad_maximum_fusion.2.x_ref, bf16[768,128]{1,0:T(8,128)(2,1)} %copy-done.1, bf16[768,50304]{1,0:T(8,128)(2,1)} %w_any.1, bf16[768,50304]{1,0:T(8,128)(2,1)} %w_any.1), custom_call_target="tpu_custom_call" | custom-call | flops 474728103936 | bytes 100000000 | tf_op jit(solution)/shard_map/heads/pallas_call | solution.py:276
  865.3 28.6 %fusion.70 = (f32[1536]{0:T(1024)S(1)}, bf16[1536,768]{1,0:T(8,128)(2,1)}) fusion(bf16[1536,768]{1,0:T(8,128)(2,1)} %copy-done.65, f32[768]{0:T(1024)S(1)} %copy-done.60, bf16[768,3072]{1,0:T(8,128)(2,1)} %param.21, f32[1536,3072]{1,0:T(8,128)} %fusion.107, bf16[3072,768]{1,0:T(8,128)(2,1)} %param.22, bf16[1536,768]{1,0:T(8,128)(2,1)} %copy-done.14, ...), kind=kOutput, calls=%fused_computation.141 | convolution fusion | flops 14615836672 | bytes 37773312 | tf_op jit(solution)/shard_map/dot_general | solution.py:39
  907.5 22.7 %fusion.13 = bf16[1536,3072]{1,0:T(8,128)(2,1)} fusion(f32[1536,3072]{1,0:T(8,128)} %fusion.92, bf16[1536,768]{1,0:T(8,128)(2,1)S(1)} %fusion.109, bf16[2,1,3072,768]{3,2,1,0:T(8,128)(2,1)} %all-gather.13.cloned.1.call-done), kind=kOutput, calls=%fused_computation.32 | convolution fusion | flops 7351566336 | bytes 35389440 | tf_op jit(solution)/shard_map/dot_general | solution.py:39
  930.3 11.7 fusion.65
  943.6 22.6 %fusion.18 = bf16[1536,3072]{1,0:T(8,128)(2,1)} fusion(f32[1536,3072]{1,0:T(8,128)} %fusion.89, bf16[1536,768]{1,0:T(8,128)(2,1)S(1)} %add_convert_fusion.1, bf16[2,1,3072,768]{3,2,1,0:T(8,128)(2,1)} %all-gather.13.cloned.1.call-done), kind=kOutput, calls=%fused_computation.37 | convolution fusion | flops 7351566336 | bytes 35389440 | tf_op jit(solution)/shard_map/dot_general | solution.py:39
  966.2 11.7 fusion.50
  993.5 13.7 convolution_bitcast_fusion
  1007.2 16.5 %convolution_bitcast_fusion.1 = f32[1,3072,768]{2,1,0:T(8,128)} fusion(bf16[1536,768]{1,0:T(8,128)(2,1)S(1)} %copy-done.21, f32[1536,3072]{1,0:T(8,128)} %fusion.89), kind=kOutput, calls=%fused_computation.113 | convolution fusion | flops 7290224640 | bytes 30670848 | tf_op jit(solution)/shard_map/dot_general | solution.py:43
  1023.7 10.8 pad_maximum_fusion.1
  1034.5 11.2 convolution_bitcast_fusion.3
  1045.8 10.9 convolution_bitcast_fusion.2
  1064.4 101.3 %all-gather.9.cloned.1.call-done.src_a = bf16[12288,768]{1,0:T(8,128)(2,1)} async-done(((bf16[3072,768]{1,0:T(8,128)(2,1)}), bf16[12288,768]{1,0:T(8,128)(2,1)}) %all-gather.9.cloned.1.call-update) | async-done | bytes 18874384 | tf_op jit(solution)/shard_map/all_gather | solution.py:514
  1167.1 33.2 %reduce-scatter.3.cloned.1.call-done = f32[1,768,3072]{2,1,0:T(8,128)} async-done(((f32[2,768,3072]{2,1,0:T(8,128)}), f32[1,768,3072]{2,1,0:T(8,128)}) %reduce-scatter.3.cloned.1.call-update) | async-done | bytes 9437200 | tf_op jit(solution)/shard_map/reduce_scatter | solution.py:524
  1200.3 28.2 %reduce-scatter.5.cloned.1.call-done = f32[1,3072,768]{2,1,0:T(8,128)} async-done(((f32[2,3072,768]{2,1,0:T(8,128)}), f32[1,3072,768]{2,1,0:T(8,128)}) %reduce-scatter.5.cloned.1.call-update) | async-done | bytes 9437200 | tf_op jit(solution)/shard_map/reduce_scatter | solution.py:525
  1274.1 23.5 %psum.21 = f32[]{:T(128)} all-reduce(f32[]{:T(128)} %multiply_reduce_fusion), channel_id=1, replica_groups=mesh['dp'=4,'pp'=2] {'dp','pp'}, use_global_device_ids=true, to_apply=%region_12.13 | all-reduce | flops 1 | bytes 8 | tf_op jit(solution)/shard_map/psum | solution.py:528
  1312.0 168.4 %table.1 = f32[1,50304,768]{2,1,0:T(8,128)} custom-call(s32[357]{0:T(512)S(1)} %broadcast_minimum_fusion.blk, s32[357]{0:T(512)S(1)} %convert_reduce_fusion.4.first, s32[1]{0:T(128)} %bitcast.16.n_groups, s32[5712]{0:T(1024)S(1)} %broadcast_add_fusion.1.sched_a, s32[5712]{0:T(1024)S(1)} %broadcast_add_fusion.sched_b, ...), custom_call_target="tpu_custom_call" | custom-call | flops 60000002048 | bytes 200000000 | tf_op jit(solution)/shard_map/table/pallas_call | solution.py:353
  1480.4 83.8 %all-reduce.8.cloned.1.call-done = (f32[1,1,768,3072]{3,2,1,0:T(8,128)}, f32[1,1,3072,768]{3,2,1,0:T(8,128)}) async-done(((f32[1,1,768,3072]{3,2,1,0:T(8,128)}, f32[1,1,3072,768]{3,2,1,0:T(8,128)}), (f32[1,1,768,3072]{3,2,1,0:T(8,128)}, f32[1,1,3072,768]{3,2,1,0:T(8,128)})) %all-reduce.8.cloned.1.call-update) | async-done | bytes 18874384 | tf_op jit(solution)/shard_map/psum | solution.py:526
  (284 shorter events, 202.6 us)
Async XLA Ops:
  7.2 177.9 %copy-start = (bf16[1536,768]{1,0:T(8,128)(2,1)S(1)}, bf16[1536,768]{1,0:T(8,128)(2,1)}, u32[]{:S(2)}) copy-start(bf16[1536,768]{1,0:T(8,128)(2,1)} %param.20) | copy-start | bytes 7077892
  7.2 116.0 %all-gather.11.cloned.1.call-start = ((), (), s32[]{:S(2)}) async-start(), calls=%async_computation.5 | async-start | bytes 14155776 | tf_op jit(solution)/shard_map/all_gather | solution.py:463
  7.9 129.1 %all-gather.13.cloned.1.call-start = ((), (), s32[]{:S(2)}) async-start(), calls=%async_computation.6 | async-start | bytes 14155776 | tf_op jit(solution)/shard_map/all_gather | solution.py:464
  8.7 1157.1 %all-gather.9.cloned.1.call-start = ((), (), s32[]{:S(2)}) async-start(), calls=%async_computation.2 | async-start | bytes 23592960 | tf_op jit(solution)/shard_map/all_gather | solution.py:514
  16.4 54.2 %copy-start.1 = (bf16[768,128]{1,0:T(8,128)(2,1)}, bf16[768,128]{1,0:T(8,128)(2,1)S(1)}, u32[]{:S(2)}) copy-start(bf16[768,128]{1,0:T(8,128)(2,1)S(1)} %slice.123.wt_ref) | copy-start | bytes 589828
  76.5 12.2 collective-permute-start
  84.2 135.8 %copy-start.24 = (f32[768]{0:T(1024)}, f32[768]{0:T(1024)S(1)}, u32[]{:S(2)}) copy-start(f32[768]{0:T(1024)S(1)} %convert_element_type.271) | copy-start | bytes 9220
  84.2 100.0 %copy-start.33 = (f32[768]{0:T(1024)}, f32[768]{0:T(1024)S(1)}, u32[]{:S(2)}) copy-start(f32[768]{0:T(1024)S(1)} %convert_element_type.273) | copy-start | bytes 9220
  84.2 36.7 %copy-start.35 = (f32[768]{0:T(1024)}, f32[768]{0:T(1024)S(1)}, u32[]{:S(2)}) copy-start(f32[768]{0:T(1024)S(1)} %convert_element_type.278) | copy-start | bytes 9220
  84.2 107.5 %copy-start.59 = (f32[768]{0:T(1024)}, f32[768]{0:T(1024)S(1)}, u32[]{:S(2)}) copy-start(f32[768]{0:T(1024)S(1)} %convert_element_type.282) | copy-start | bytes 9220
  101.8 19.1 %copy-start.26 = (f32[1536]{0:T(1024)}, f32[1536]{0:T(1024)S(1)}, u32[]{:S(2)}) copy-start(f32[1536]{0:T(1024)S(1)} %rsqrt.71) | copy-start | bytes 18436
  185.0 37.0 %copy-start.10 = (bf16[1536,768]{1,0:T(8,128)(2,1)}, bf16[1536,768]{1,0:T(8,128)(2,1)S(1)}, u32[]{:S(2)}) copy-start(bf16[1536,768]{1,0:T(8,128)(2,1)S(1)} %get-tuple-element.47) | copy-start | bytes 7077892
  225.9 626.9 %copy-start.51 = (f32[3072]{0:T(1024)S(1)}, f32[3072]{0:T(1024)}, u32[]{:S(2)}) copy-start(f32[3072]{0:T(1024)} %constant.125.clone.1) | copy-start | bytes 36868
  865.3 28.6 %copy-start.47 = (f32[1536]{0:T(1024)S(1)}, f32[1536]{0:T(1024)}, u32[]{:S(2)}) copy-start(f32[1536]{0:T(1024)} %copy-done.46) | copy-start | bytes 18436
  865.3 28.6 %copy-start.58 = (f32[1536]{0:T(1024)S(1)}, f32[1536]{0:T(1024)}, u32[]{:S(2)}) copy-start(f32[1536]{0:T(1024)} %copy-done.57) | copy-start | bytes 18436
  907.5 34.5 %copy-start.13 = (bf16[1536,768]{1,0:T(8,128)(2,1)}, bf16[1536,768]{1,0:T(8,128)(2,1)S(1)}, u32[]{:S(2)}) copy-start(bf16[1536,768]{1,0:T(8,128)(2,1)S(1)} %fusion.109) | copy-start | bytes 7077892
  907.5 22.7 %copy-start.18 = (bf16[1536,768]{1,0:T(8,128)(2,1)S(1)}, bf16[1536,768]{1,0:T(8,128)(2,1)}, u32[]{:S(2)}) copy-start(bf16[1536,768]{1,0:T(8,128)(2,1)} %copy-done.17) | copy-start | bytes 7077892
  943.6 38.1 %copy-start.20 = (bf16[1536,768]{1,0:T(8,128)(2,1)}, bf16[1536,768]{1,0:T(8,128)(2,1)S(1)}, u32[]{:S(2)}) copy-start(bf16[1536,768]{1,0:T(8,128)(2,1)S(1)} %add_convert_fusion.1) | copy-start | bytes 7077892
  993.5 206.8 %reduce-scatter.3.cloned.1.call-start = ((), (), s32[]{:S(2)}) async-start(), calls=%async_computation.3 | async-start | bytes 28311552 | tf_op jit(solution)/shard_map/reduce_scatter | solution.py:524
  1063.8 164.6 %reduce-scatter.5.cloned.1.call-start = ((), (), s32[]{:S(2)}) async-start(), calls=%async_computation.4 | async-start | bytes 28311552 | tf_op jit(solution)/shard_map/reduce_scatter | solution.py:525
  1064.4 499.8 %all-reduce.8.cloned.1.call-start = ((), (), s32[]{:S(2)}) async-start(), calls=%async_computation.7 | async-start | bytes 37748736 | tf_op jit(solution)/shard_map/psum | solution.py:526
  1165.8 131.8 %collective-permute-start.1 = (bf16[12288,768]{1,0:T(8,128)(2,1)}, bf16[12288,768]{1,0:T(8,128)(2,1)}, u32[]{:S(2)}, u32[]{:S(2)}) collective-permute-start(bf16[12288,768]{1,0:T(8,128)(2,1)} %all-gather.9.cloned.1.call-done.src_a), channel_id=1, source_target_pairs={{1,0},{3,2},{5,4},{7,6}} | collective-permute-start | bytes 56623112 | tf_op jit(solution)/shard_map/ppermute | solution.py:515
  1228.5 37.8 %copy-start.23 = (f32[3072]{0:T(1024)S(1)}, f32[3072]{0:T(1024)}, u32[]{:S(2)}) copy-start(f32[3072]{0:T(1024)} %copy-done.22) | copy-start | bytes 36868
  1228.5 39.5 %copy-start.37 = (f32[3072]{0:T(1024)S(1)}, f32[3072]{0:T(1024)}, u32[]{:S(2)}) copy-start(f32[3072]{0:T(1024)} %get-tuple-element.41) | copy-start | bytes 36868
  (57 other events, 397.1 us)
Sparse Core Ops, SparseCore 0:
  9.5 22.6 all-gather.10
  33.7 20.9 all-gather.12
  993.6 172.1 all-gather.8
  1168.5 31.7 reduce-scatter.2
  1202.4 25.9 reduce-scatter.4
  1232.0 332.1 all-reduce.7
